TPU v7x, 32 devices: a whole 2x2x4 slice. The times are simulated.
32 devices in a mesh: rep: 4 (over y, x), fsdp: 8 (over z, core).
Axes of the slice: x: 2, y: 2, z: 4, core: 2. Of those that a mesh axis runs over, the one named last changes fastest.
Arguments:
- latents: bfloat16 [8, 1024, 1152], P('fsdp', 'rep'), may hold values from -6 to 6
- condition: bfloat16 [8, 1152], P('fsdp'), may hold values from -6 to 6
- adapter_index: int32 [8, 5], P('fsdp'), may hold values from 0 to 7
- weight_mod: bfloat16 [1152, 6912], P('fsdp'), may hold values from -0.1875 to 0.1875
- weight_qkv: bfloat16 [1152, 3456], P('fsdp'), may hold values from -0.1875 to 0.1875
- weight_proj: bfloat16 [1152, 1152], P('fsdp'), may hold values from -3 to 3
- weight_fc1: bfloat16 [1152, 4608], P('fsdp'), may hold values from -0.1875 to 0.1875
- weight_fc2: bfloat16 [4608, 1152], P('fsdp'), may hold values from -0.09375 to 0.09375
- master: float32 [3391488], P('fsdp'), may hold values from -0.25 to 0.25
- moment1: float32 [3391488], P('fsdp'), may hold values from -64 to 64
- moment2: float32 [3391488], P('fsdp'), may hold values from 1 to 1000
- cotangent: bfloat16 [8, 1024, 1152], P('fsdp', 'rep'), may hold values from -6 to 6
Outputs:
- output: bfloat16 [8, 1024, 1152], P('fsdp', 'rep')
- latents_grad: float32 [8, 1024, 1152], P('fsdp', 'rep')
- condition_grad: float32 [8, 1152], P('fsdp')
- new_master: float32 [3391488], P('fsdp')
- new_moment1: float32 [3391488], P('fsdp')
- new_moment2: float32 [3391488], P('fsdp')
- rounded_adapters: bfloat16 [3391488], P('fsdp')
All inputs are finite; a program needn't handle non-finite values.
Results may differ from a plain program's by a relative error of at most 0.03.
The roundings to bfloat16 on the way count: a program that leaves them out, or rounds other values in their place, can miss the bound.
Values may be sent and summed in bfloat16 or wider, within the bound.
A program may use at most 256 MiB of HBM per device.

v0:
```python
import jax
import jax.numpy as jnp
from jax import lax
from jax.sharding import PartitionSpec as P

D = 1152
HEAD_DIM = 72
FF = 4608
RANK = 16
ADAPT = 8
STEP = 3
adapter_scale = 2.0
norm_eps = 1e-06


def adapter_shapes():
    pairs = [(D, 6 * D), (D, 3 * D), (D, D), (D, FF), (FF, D)]
    shapes = []
    for fan_in, fan_out in pairs:
        shapes.append((ADAPT, fan_in, RANK))
        shapes.append((ADAPT, RANK, fan_out))
    return shapes


def unpack(flat):
    tables = []
    offset = 0
    for shape in adapter_shapes():
        count = shape[0] * shape[1] * shape[2]
        tables.append(flat[offset : offset + count].reshape(shape))
        offset = offset + count
    return tables


def norm_modulate(values, shift, scale):
    centred = values - jnp.mean(values, axis=-1, keepdims=True)
    spread = jnp.mean(centred * centred, axis=-1, keepdims=True)
    normed = centred * lax.rsqrt(spread + norm_eps)
    return normed * (1.0 + scale[:, None, :]) + shift[:, None, :]


def gelu_tanh(values):
    return jax.nn.gelu(values, approximate=True)


def shards(
    latents,
    condition,
    adapter_index,
    weight_mod,
    weight_qkv,
    weight_proj,
    weight_fc1,
    weight_fc2,
    master,
    moment1,
    moment2,
    cotangent,
):
    maximal_precision = lax.Precision.HIGHEST
    seqs, tokens, width = latents.shape
    heads = width // HEAD_DIM
    scale = HEAD_DIM ** (-0.5)
    adapters = lax.all_gather(master.astype(jnp.bfloat16), "fsdp", axis=0, tiled=True)
    tables = unpack(adapters)
    select = jax.nn.one_hot(adapter_index, ADAPT, dtype=jnp.float32)
    select_low = select.astype(jnp.bfloat16)
    downs = [
        jnp.einsum(
            "sk,kdr->sdr",
            select_low[:, selected_adapter],
            tables[2 * selected_adapter],
            preferred_element_type=jnp.float32,
        ).astype(jnp.bfloat16)
        for selected_adapter in range(5)
    ]
    raise_factors = [
        jnp.einsum(
            "sk,kro->sro",
            select_low[:, selected_adapter],
            tables[2 * selected_adapter + 1],
            preferred_element_type=jnp.float32,
        ).astype(jnp.bfloat16)
        for selected_adapter in range(5)
    ]

    def adapted(rows_low, weight, selected_adapter):
        inner_lowrank = jnp.einsum(
            "std,sdr->str", rows_low, downs[selected_adapter], preferred_element_type=jnp.float32
        ).astype(jnp.bfloat16)
        additional_term = adapter_scale * jnp.einsum(
            "str,sro->sto",
            inner_lowrank,
            raise_factors[selected_adapter],
            preferred_element_type=jnp.float32,
        )
        return (
            jnp.einsum("std,de->ste", rows_low, weight, preferred_element_type=jnp.float32)
            + additional_term,
            inner_lowrank,
        )

    def adapted_back(grad_low, weight, rows_low, inner_lowrank, selected_adapter):
        raise_gradient = adapter_scale * jnp.einsum(
            "str,sto->sro", inner_lowrank, grad_low, preferred_element_type=jnp.float32
        )
        grad_inner = (
            adapter_scale
            * jnp.einsum(
                "sto,sro->str",
                grad_low,
                raise_factors[selected_adapter],
                preferred_element_type=jnp.float32,
            )
        ).astype(jnp.bfloat16)
        grad_down = jnp.einsum(
            "std,str->sdr", rows_low, grad_inner, preferred_element_type=jnp.float32
        )
        grad_rows = jnp.einsum("ste,de->std", grad_low, weight, preferred_element_type=jnp.float32)
        grad_rows = grad_rows + jnp.einsum(
            "str,sdr->std", grad_inner, downs[selected_adapter], preferred_element_type=jnp.float32
        )
        return (grad_rows, grad_down, raise_gradient)

    cond_full = condition.astype(jnp.float32)
    condition_activated, silu_back = jax.vjp(jax.nn.silu, cond_full)
    silu_low = condition_activated.astype(jnp.bfloat16)
    apply_modulation = jnp.dot(
        silu_low,
        lax.all_gather(weight_mod, "fsdp", axis=0, tiled=True),
        preferred_element_type=jnp.float32,
    )
    inner_modulation = jnp.einsum(
        "sd,sdr->sr", silu_low, downs[0], preferred_element_type=jnp.float32
    ).astype(jnp.bfloat16)
    apply_modulation = apply_modulation + adapter_scale * jnp.einsum(
        "sr,sro->so", inner_modulation, raise_factors[0], preferred_element_type=jnp.float32
    )
    shift_a, scale_a, gate_a, shift_m, scale_m, gate_m = jnp.split(apply_modulation, 6, axis=1)
    attn_weight, proj_weight = (
        lax.all_gather(weight_qkv, "fsdp", axis=0, tiled=True),
        lax.all_gather(weight_proj, "fsdp", axis=0, tiled=True),
    )
    residual_in = latents.astype(jnp.float32)
    first, first_back = jax.vjp(norm_modulate, residual_in, shift_a, scale_a)
    first_low = first.astype(jnp.bfloat16)
    qkv, inner_qkv = adapted(first_low, attn_weight, 1)
    qkv_low = qkv.astype(jnp.bfloat16)
    query = qkv_low[..., :width]
    keys = qkv_low[..., width : 2 * width]
    values = qkv_low[..., 2 * width :]
    keys_all, values_all = (
        lax.all_gather(keys, "rep", axis=1, tiled=True),
        lax.all_gather(values, "rep", axis=1, tiled=True),
    )
    length = keys_all.shape[1]
    latent = 0
    query_heads = query[latent].reshape(tokens, heads, HEAD_DIM)
    key_heads = keys_all[latent].reshape(length, heads, HEAD_DIM)
    value_heads = values_all[latent].reshape(length, heads, HEAD_DIM)
    scores = (
        jnp.einsum("qhe,khe->hqk", query_heads, key_heads, preferred_element_type=jnp.float32)
        * scale
    )
    log_total = jax.nn.logsumexp(scores, axis=-1, keepdims=True)
    probs_low = jnp.exp(scores - log_total).astype(jnp.bfloat16)
    mixed_rows = [
        jnp.einsum(
            "hqk,khe->qhe", probs_low, value_heads, preferred_element_type=jnp.float32
        ).reshape(tokens, width)
    ]
    lse_rows = [log_total]
    mixed_low = jnp.stack(mixed_rows).astype(jnp.bfloat16)
    attn_out, inner_proj = adapted(mixed_low, proj_weight, 2)
    after_attn = residual_in + gate_a[:, None] * attn_out
    expand = lax.all_gather(weight_fc1, "fsdp", axis=0, tiled=True)
    second, second_back = jax.vjp(norm_modulate, after_attn, shift_m, scale_m)
    second_low = second.astype(jnp.bfloat16)
    pre, inner_fc1 = adapted(second_low, expand, 3)
    act, gelu_back = jax.vjp(gelu_tanh, pre)
    act_low = act.astype(jnp.bfloat16)
    contract = lax.all_gather(weight_fc2, "fsdp", axis=0, tiled=True)
    mlp_out, inner_fc2 = adapted(act_low, contract, 4)
    result = after_attn + gate_m[:, None] * mlp_out
    grad_out = cotangent.astype(jnp.float32)
    grad_downs = [None] * 5
    raise_gradient_list = [None] * 5
    d_gate_m = jnp.sum(grad_out * mlp_out, axis=1)
    d_mlp = (grad_out * gate_m[:, None]).astype(jnp.bfloat16)
    d_act, grad_downs[4], raise_gradient_list[4] = adapted_back(
        d_mlp, contract, act_low, inner_fc2, 4
    )
    d_pre = gelu_back(d_act)[0].astype(jnp.bfloat16)
    d_second, grad_downs[3], raise_gradient_list[3] = adapted_back(
        d_pre, expand, second_low, inner_fc1, 3
    )
    d_after, d_shift_m, d_scale_m = second_back(d_second)
    d_after = grad_out + d_after
    d_gate_a = jnp.sum(d_after * attn_out, axis=1)
    d_attn = (d_after * gate_a[:, None]).astype(jnp.bfloat16)
    d_mixed, grad_downs[2], raise_gradient_list[2] = adapted_back(
        d_attn, proj_weight, mixed_low, inner_proj, 2
    )
    d_mixed_low = d_mixed.astype(jnp.bfloat16)
    latent = 0
    query_heads = query[latent].reshape(tokens, heads, HEAD_DIM)
    key_heads = keys_all[latent].reshape(length, heads, HEAD_DIM)
    value_heads = values_all[latent].reshape(length, heads, HEAD_DIM)
    grad_heads = d_mixed_low[latent].reshape(tokens, heads, HEAD_DIM)
    scores = (
        jnp.einsum("qhe,khe->hqk", query_heads, key_heads, preferred_element_type=jnp.float32)
        * scale
    )
    probs = jnp.exp(scores - lse_rows[latent])
    probs_low = probs.astype(jnp.bfloat16)
    d_value_rows = [
        jnp.einsum(
            "hqk,qhe->khe", probs_low, grad_heads, preferred_element_type=jnp.float32
        ).reshape(length, width)
    ]
    d_probs = jnp.einsum(
        "qhe,khe->hqk", grad_heads, value_heads, preferred_element_type=jnp.float32
    )
    centre = jnp.sum(probs * d_probs, axis=-1, keepdims=True)
    d_scores = (probs * (d_probs - centre)).astype(jnp.bfloat16)
    d_query_rows = [
        (
            jnp.einsum("hqk,khe->qhe", d_scores, key_heads, preferred_element_type=jnp.float32)
            * scale
        ).reshape(tokens, width)
    ]
    d_key_rows = [
        (
            jnp.einsum("hqk,qhe->khe", d_scores, query_heads, preferred_element_type=jnp.float32)
            * scale
        ).reshape(length, width)
    ]
    d_keys, d_values = (
        lax.psum_scatter(
            jnp.stack(d_key_rows).astype(jnp.bfloat16), "rep", scatter_dimension=1, tiled=True
        ).astype(jnp.float32),
        lax.psum_scatter(
            jnp.stack(d_value_rows).astype(jnp.bfloat16), "rep", scatter_dimension=1, tiled=True
        ).astype(jnp.float32),
    )
    d_qkv = jnp.concatenate([jnp.stack(d_query_rows), d_keys, d_values], axis=-1).astype(
        jnp.bfloat16
    )
    d_first, grad_downs[1], raise_gradient_list[1] = adapted_back(
        d_qkv, attn_weight, first_low, inner_qkv, 1
    )
    d_input, d_shift_a, d_scale_a = first_back(d_first)
    latents_grad = d_after + d_input
    modulation_partial = jnp.concatenate(
        [d_shift_a, d_scale_a, d_gate_a, d_shift_m, d_scale_m, d_gate_m], axis=1
    )
    raise_modulation = raise_factors[0].astype(jnp.float32)
    down_mod = downs[0].astype(jnp.float32)
    raise_gradient_list[0] = adapter_scale * jnp.einsum(
        "sr,so->sro",
        inner_modulation.astype(jnp.float32),
        modulation_partial,
        precision=maximal_precision,
    )
    inner_portion = adapter_scale * jnp.einsum(
        "gi,gwi->gw", modulation_partial, raise_modulation, precision=maximal_precision
    )
    grad_downs[0] = jnp.einsum(
        "sd,sr->sdr", silu_low.astype(jnp.float32), inner_portion, precision=maximal_precision
    )
    modulation_total = lax.psum(modulation_partial, "rep")
    d_silu = jnp.dot(
        modulation_total,
        lax.all_gather(weight_mod, "fsdp", axis=0, tiled=True).astype(jnp.float32).T,
        precision=maximal_precision,
    )
    inner_combined = adapter_scale * jnp.einsum(
        "gi,gwi->gw", modulation_total, raise_modulation, precision=maximal_precision
    )
    d_silu = d_silu + jnp.einsum(
        "sr,sdr->sd", inner_combined, down_mod, precision=maximal_precision
    )
    condition_grad = silu_back(d_silu)[0]
    pieces = []
    for selected_adapter in range(5):
        pieces.append(
            jnp.einsum(
                "sk,sdr->kdr",
                select[:, selected_adapter],
                grad_downs[selected_adapter],
                precision=maximal_precision,
            ).reshape(-1)
        )
        pieces.append(
            jnp.einsum(
                "sk,sro->kro",
                select[:, selected_adapter],
                raise_gradient_list[selected_adapter],
                precision=maximal_precision,
            ).reshape(-1)
        )
    flat_grad = jnp.concatenate(pieces)
    grad = lax.psum_scatter(
        flat_grad.astype(jnp.bfloat16), "fsdp", scatter_dimension=0, tiled=True
    ).astype(jnp.float32)
    grad = lax.psum(grad, "rep")
    new_moment1 = 0.5 * moment1 + 0.5 * grad
    new_moment2 = 0.5 * moment2 + 0.5 * grad * grad
    first_hat = new_moment1 / (1.0 - 0.5**STEP)
    second_hat = new_moment2 / (1.0 - 0.5**STEP)
    new_master = master - 0.01 * (first_hat / (jnp.sqrt(second_hat) + 1e-08) + 0.1 * master)
    return (
        result.astype(jnp.bfloat16),
        latents_grad,
        condition_grad,
        new_master,
        new_moment1,
        new_moment2,
        new_master.astype(jnp.bfloat16),
    )


def solution(mesh):
    return jax.shard_map(
        shards,
        mesh=mesh,
        in_specs=(
            P("fsdp", "rep", None),
            P("fsdp", None),
            P("fsdp", None),
            P("fsdp", None),
            P("fsdp", None),
            P("fsdp", None),
            P("fsdp", None),
            P("fsdp", None),
            P("fsdp"),
            P("fsdp"),
            P("fsdp"),
            P("fsdp", "rep", None),
        ),
        out_specs=(
            P("fsdp", "rep", None),
            P("fsdp", "rep", None),
            P("fsdp", None),
            P("fsdp"),
            P("fsdp"),
            P("fsdp"),
            P("fsdp"),
        ),
        check_vma=False,
    )
```

profile of v0, /device:TPU:0, one launch (start us, length us, event | category | flops | bytes accessed | tf_op | source)
XLA Modules:
  0.0 1016.1 jit_solution(8816787892493126649)
XLA Ops:
  15.3 66.5 %all-gather.11.cloned.1.call-done = bf16[3391488]{0:T(1024)(128)(2,1)} async-done(((bf16[423936]{0:T(1024)(128)(2,1)}), bf16[3391488]{0:T(1024)(128)(2,1)}) %all-gather.11.cloned.1.call-update) | async-done | bytes 6782992 | tf_op jit(solution)/shard_map/all_gather | solution.py:64
  84.7 2.9 slice.191
  87.7 3.7 reshape.802
  104.7 121.4 %all-gather.9.cloned.1.call-done = bf16[1152,6912]{1,0:T(8,128)(2,1)} async-done(((bf16[144,6912]{1,0:T(8,128)(2,1)}), bf16[1152,6912]{1,0:T(8,128)(2,1)}) %all-gather.9.cloned.1.call-update) | async-done | bytes 15925264 | tf_op jit(solution)/shard_map/all_gather | solution.py:130
  226.1 7.7 convolution_reduce_fusion
  235.7 68.8 %all-gather.13.cloned.1.call-done = bf16[1152,3456]{1,0:T(8,128)(2,1)} async-done(((bf16[144,3456]{1,0:T(8,128)(2,1)}), bf16[1152,3456]{1,0:T(8,128)(2,1)}) %all-gather.13.cloned.1.call-update) | async-done | bytes 7962640 | tf_op jit(solution)/shard_map/all_gather | solution.py:141
  304.5 5.8 fusion.111
  327.2 8.3 slice.182
  335.4 6.3 multiply_reduce_fusion
  343.9 3.2 multiply_reduce_fusion.3
  352.1 52.9 %all-gather.23.cloned.1.call-done = bf16[4608,1152]{1,0:T(8,128)(2,1)} async-done(((bf16[576,1152]{1,0:T(8,128)(2,1)}), bf16[4608,1152]{1,0:T(8,128)(2,1)}) %all-gather.23.cloned.1.call-update) | async-done | bytes 10616848 | tf_op jit(solution)/shard_map/all_gather | solution.py:182
  405.0 12.3 %fusion.56 = f32[256,4608]{1,0:T(8,128)} fusion(bf16[4608,1152]{1,0:T(8,128)(2,1)} %all-gather.23.cloned.1.call-done, bf16[1,256,1152]{2,1,0:T(8,128)(2,1)S(1)} %copy-done.13, f32[1152]{0:T(1024)S(1)} %get-tuple-element.13), kind=kOutput, calls=%fused_computation.129 | convolution fusion | flops 2718793728 | bytes 15929856 | tf_op jit(solution)/shard_map/ste,de->std/dot_general | solution.py:119
  417.3 25.6 %all-gather.17.cloned.1.call-done = bf16[1,1024,1152]{2,1,0:T(8,128)(2,1)} async-done(((bf16[1,256,1152]{2,1,0:T(8,128)(2,1)}), bf16[1,1024,1152]{2,1,0:T(8,128)(2,1)}) %all-gather.17.cloned.1.call-update) | async-done | bytes 2359312 | tf_op jit(solution)/shard_map/all_gather | solution.py:153
  442.9 4.3 copy.49
  447.2 35.3 %all-gather.15.cloned.1.call-done = bf16[1,1024,1152]{2,1,0:T(8,128)(2,1)} async-done(((bf16[1,256,1152]{2,1,0:T(8,128)(2,1)}), bf16[1,1024,1152]{2,1,0:T(8,128)(2,1)}) %all-gather.15.cloned.1.call-update) | async-done | bytes 2359312 | tf_op jit(solution)/shard_map/all_gather | solution.py:154
  482.6 4.7 copy.47
  487.3 4.2 multiply_reduce_fusion.2
  491.5 3.7 exponential_reduce_fusion
  497.9 3.9 convolution_convert_fusion.1
  502.7 15.6 %all-gather.19.cloned.1.call-done = bf16[1152,1152]{1,0:T(8,128)(2,1)} async-done(((bf16[144,1152]{1,0:T(8,128)(2,1)}), bf16[1152,1152]{1,0:T(8,128)(2,1)}) %all-gather.19.cloned.1.call-update) | async-done | bytes 2654224 | tf_op jit(solution)/shard_map/all_gather | solution.py:142
  518.3 2.8 fusion.112
  523.8 95.7 %all-gather.21.cloned.1.call-done = bf16[1152,4608]{1,0:T(8,128)(2,1)} async-done(((bf16[144,4608]{1,0:T(8,128)(2,1)}), bf16[1152,4608]{1,0:T(8,128)(2,1)}) %all-gather.21.cloned.1.call-update) | async-done | bytes 10616848 | tf_op jit(solution)/shard_map/all_gather | solution.py:176
  619.5 5.9 fusion.113
  627.7 6.4 fusion.11
  636.0 3.2 fusion.115
  649.6 10.5 %convolution_convert_fusion = bf16[16,72,1024]{2,1,0:T(8,128)(2,1)} fusion(bf16[256,16,72]{0,2,1:T(8,128)(2,1)} %bitcast.241, f32[16,256,1024]{2,1,0:T(8,128)} %copy-done, f32[16,256]{1,0:T(8,128)S(1)} %log_add_fusion), kind=kOutput, calls=%fused_computation.50 | convolution fusion | flops 617742336 | bytes 19742720 | tf_op jit(solution)/shard_map/hqk,qhe->khe/dot_general | solution.py:217
  660.1 12.9 %multiply_reduce_fusion.1 = (f32[16,256]{1,0:T(8,128)S(1)}, f32[16,256,1024]{2,1,0:T(8,128)}) fusion(f32[16,256,1024]{2,1,0:T(8,128)} %copy-done, f32[16,256]{1,0:T(8,128)S(1)} %log_add_fusion, bf16[256,16,72]{0,2,1:T(8,128)(2,1)} %bitcast.242, bf16[1024,16,72]{0,2,1:T(8,128)(2,1)} %bitcast.232), kind=kOutput, calls=%fused_computation.3 | convolution fusion | flops 620752896 | bytes 36536320 | tf_op jit(solution)/shard_map/qhe,khe->hqk/dot_general | solution.py:221
  673.1 12.3 %multiply_convert_fusion.1 = bf16[16,256,1024]{2,1,0:T(8,128)(2,1)S(1)} fusion(f32[16,256,1024]{2,1,0:T(8,128)} %get-tuple-element.61, f32[16,256,1024]{2,1,0:T(8,128)} %copy-done, f32[16,256]{1,0:T(8,128)S(1)} %get-tuple-element.60, f32[16,256]{1,0:T(8,128)S(1)} %log_add_fusion), kind=kLoop, calls=%fused_computation.2 | loop fusion | flops 20971520 | bytes 41975808 | tf_op jit(solution)/shard_map/convert_element_type | solution.py:225
  685.4 3.5 multiply_convert_fusion.6
  696.5 3.7 reshape.825
  700.9 3.2 multiply_convert_fusion.2
  704.1 3.9 reshape.824
  708.0 3.9 reshape.821
  714.5 5.2 multiply_convert_fusion
  719.8 11.3 %reshape.827 = bf16[589824]{0:T(1024)(128)(2,1)} reshape(bf16[8,4608,16]{2,1,0:T(8,128)(2,1)} %multiply_convert_fusion) | data formatting | bytes 2359296 | tf_op jit(solution)/shard_map/reshape | solution.py:292
  731.0 7.0 fusion.24
  738.1 7.2 fusion.114
  749.6 5.9 fusion.101
  759.6 4.0 fusion.33
  768.1 3.6 reshape.816
  771.9 3.5 multiply_convert_fusion.4
  775.4 3.5 reshape.818
  782.8 2.9 constant_dynamic-update-slice_fusion.15
  794.5 142.3 %all-reduce.6.cloned.1.call-done = bf16[3391488]{0:T(1024)(128)(2,1)} async-done(((bf16[3391488]{0:T(1024)(128)(2,1)}), bf16[3391488]{0:T(1024)(128)(2,1)}) %all-reduce.6.cloned.1.call-update) | async-done | bytes 6782992
  939.3 16.9 %psum.14 = f32[6912]{0:T(1024)S(1)} all-reduce(f32[6912]{0:T(1024)S(1)} %copy-done.55), channel_id=1, replica_groups=mesh['rep'=4,'fsdp'=8] {'rep'}, use_global_device_ids=true, to_apply=%region_19.20 | all-reduce | flops 6912 | bytes 55296 | tf_op jit(solution)/shard_map/psum | solution.py:271
  957.0 15.4 %convolution_reduce_fusion.3 = f32[1152]{0:T(1024)S(1)} fusion(f32[6912,1]{0,1:T(1,128)S(1)} %reshape.860, bf16[1152,6912]{1,0:T(8,128)(2,1)} %all-gather.9.cloned.1.call-done), kind=kOutput, calls=%fused_computation.110 | convolution fusion | flops 95551488 | bytes 15957504 | tf_op jit(solution)/shard_map/dot_general | solution.py:272
  973.1 30.4 %all-reduce.4.cloned.1.call-done = f32[423936]{0:T(1024)} async-done(((f32[423936]{0:T(1024)}), f32[423936]{0:T(1024)}) %all-reduce.4.cloned.1.call-update) | async-done | bytes 1695760 | tf_op jit(solution)/shard_map/psum | solution.py:306
  1003.6 5.5 fusion.103
  (381 shorter events, 109.9 us)
Async XLA Ops:
  7.2 74.5 %all-gather.11.cloned.1.call-start = ((), (), s32[]{:S(2)}) async-start(), calls=%async_computation.3 | async-start | bytes 7630848 | tf_op jit(solution)/shard_map/all_gather | solution.py:64
  9.7 216.4 %all-gather.9.cloned.1.call-start = ((), (), s32[]{:S(2)}) async-start(), calls=%async_computation.2 | async-start | bytes 17915904 | tf_op jit(solution)/shard_map/all_gather | solution.py:130
  10.5 294.0 %all-gather.13.cloned.1.call-start = ((), (), s32[]{:S(2)}) async-start(), calls=%async_computation.4 | async-start | bytes 8957952 | tf_op jit(solution)/shard_map/all_gather | solution.py:141
  11.2 393.8 %all-gather.23.cloned.1.call-start = ((), (), s32[]{:S(2)}) async-start(), calls=%async_computation.9 | async-start | bytes 11943936 | tf_op jit(solution)/shard_map/all_gather | solution.py:182
  11.8 431.2 %all-gather.17.cloned.1.call-start = ((), (), s32[]{:S(2)}) async-start(), calls=%async_computation.6 | async-start | bytes 2949120 | tf_op jit(solution)/shard_map/all_gather | solution.py:153
  12.0 222.5 %copy-start.78 = (f32[256]{0:T(256)}, f32[256]{0:T(256)S(1)}, u32[]{:S(2)}) copy-start(f32[256]{0:T(256)S(1)} %broadcast_multiply_fusion.2) | copy-start | bytes 3076
  12.3 72.4 %copy-start.94 = (f32[256]{0:T(256)}, f32[256]{0:T(256)S(1)}, u32[]{:S(2)}) copy-start(f32[256]{0:T(256)S(1)} %fusion.30) | copy-start | bytes 3076
  104.0 206.2 %copy-start.45 = (bf16[1,16,3456]{2,0,1:T(2,128)(2,1)}, bf16[1,16,3456]{2,0,1:T(2,128)(2,1)S(1)}, u32[]{:S(2)}) copy-start(bf16[1,16,3456]{2,0,1:T(2,128)(2,1)S(1)} %fusion.48) | copy-start | bytes 331780
  104.7 130.7 %copy-start.24 = (bf16[1152,16]{1,0:T(8,128)(2,1)}, bf16[1152,16]{1,0:T(8,128)(2,1)S(1)}, u32[]{:S(2)}) copy-start(bf16[1152,16]{1,0:T(8,128)(2,1)S(1)} %multiply_reduce_fusion.5) | copy-start | bytes 110596
  104.7 130.4 %copy-start.86 = (f32[256]{0:T(256)S(1)}, f32[256]{0:T(256)}, u32[]{:S(2)}) copy-start(f32[256]{0:T(256)} %fusion.81) | copy-start | bytes 3076
  234.5 170.5 %copy-start.69 = (f32[1152]{0:T(1024)}, f32[1152]{0:T(1024)S(1)}, u32[]{:S(2)}) copy-start(f32[1152]{0:T(1024)S(1)} %get-tuple-element.13) | copy-start | bytes 13828
  235.4 74.8 %copy-start.16 = (bf16[256,1152]{1,0:T(8,128)(2,1)}, bf16[256,1152]{1,0:T(8,128)(2,1)S(1)}, u32[]{:S(2)}) copy-start(bf16[256,1152]{1,0:T(8,128)(2,1)S(1)} %fusion.53) | copy-start | bytes 1769476
  235.7 74.6 %copy-start.80 = (bf16[256,16]{0,1:T(8,128)(2,1)}, bf16[256,16]{0,1:T(8,128)(2,1)S(1)}, u32[]{:S(2)}) copy-start(bf16[256,16]{0,1:T(8,128)(2,1)S(1)} %convolution_convert_fusion.4) | copy-start | bytes 24580
  312.3 170.3 %all-gather.15.cloned.1.call-start = ((), (), s32[]{:S(2)}) async-start(), calls=%async_computation.5 | async-start | bytes 2949120 | tf_op jit(solution)/shard_map/all_gather | solution.py:154
  312.8 205.4 %all-gather.19.cloned.1.call-start = ((), (), s32[]{:S(2)}) async-start(), calls=%async_computation.7 | async-start | bytes 2985984 | tf_op jit(solution)/shard_map/all_gather | solution.py:142
  313.6 305.9 %all-gather.21.cloned.1.call-start = ((), (), s32[]{:S(2)}) async-start(), calls=%async_computation.8 | async-start | bytes 11943936 | tf_op jit(solution)/shard_map/all_gather | solution.py:176
  314.3 431.0 %reduce-scatter.5.cloned.1.call-start = ((), (), s32[]{:S(2)}) async-start(), calls=%async_computation.11 | async-start | bytes 2949120 | tf_op jit(solution)/shard_map/reduce_scatter | solution.py:242
  327.2 8.3 copy-start.109
  335.4 7.3 copy-start.36
  335.4 7.5 copy-start.37
  343.0 8.2 copy-start.58
  347.7 154.1 %copy-start.26 = (bf16[1152,16]{1,0:T(8,128)(2,1)}, bf16[1152,16]{1,0:T(8,128)(2,1)S(1)}, u32[]{:S(2)}) copy-start(bf16[1152,16]{1,0:T(8,128)(2,1)S(1)} %multiply_reduce_fusion.4) | copy-start | bytes 110596
  491.4 6.5 copy-start
  491.5 6.4 copy-start.3
  501.8 19.3 %copy-start.11 = (bf16[16,72,256]{2,1,0:T(8,128)(2,1)}, bf16[16,72,256]{2,1,0:T(8,128)(2,1)S(1)}, u32[]{:S(2)}) copy-start(bf16[16,72,256]{2,1,0:T(8,128)(2,1)S(1)} %convolution_convert_fusion.1) | copy-start | bytes 1769476
  523.5 101.9 %copy-start.18 = (bf16[256,1152]{1,0:T(8,128)(2,1)}, bf16[256,1152]{1,0:T(8,128)(2,1)S(1)}, u32[]{:S(2)}) copy-start(bf16[256,1152]{1,0:T(8,128)(2,1)S(1)} %fusion.50) | copy-start | bytes 1769476
  523.8 101.7 %copy-start.43 = (bf16[1,16,4608]{2,0,1:T(2,128)(2,1)S(1)}, bf16[1,16,4608]{2,0,1:T(2,128)(2,1)}, u32[]{:S(2)}) copy-start(bf16[1,16,4608]{2,0,1:T(2,128)(2,1)} %fusion.38) | copy-start | bytes 442372
  625.5 10.4 %slice-start.1 = ((s8[10616832]{0:T(1024)(128)(4,1)}), s8[4194304]{0:T(1024)(128)(4,1)S(1)}, s32[]{:S(2)}) async-start(s8[10616832]{0:T(1024)(128)(4,1)} %bitcast.247), calls=%async_computation.15 | async-start | bytes 8388608
  627.6 15.4 %copy-start.4 = (bf16[256,4608]{1,0:T(8,128)(2,1)}, bf16[256,4608]{1,0:T(8,128)(2,1)S(1)}, u32[]{:S(2)}) copy-start(bf16[256,4608]{1,0:T(8,128)(2,1)S(1)} %get-tuple-element.57) | copy-start | bytes 7077892
  627.6 8.3 slice-start.2
  627.6 8.3 slice-start.3
  660.1 85.2 %reduce-scatter.3.cloned.1.call-start = ((), (), s32[]{:S(2)}) async-start(), calls=%async_computation.10 | async-start | bytes 2949120 | tf_op jit(solution)/shard_map/reduce_scatter | solution.py:239
  690.7 246.1 %all-reduce.6.cloned.1.call-start = ((), (), s32[]{:S(2)}) async-start(), calls=%async_computation.13 | async-start | bytes 13565952
  691.7 8.5 copy-start.19
  691.7 8.5 copy-start.64
  692.4 8.2 copy-start.12
  692.4 8.2 copy-start.66
  704.1 7.9 copy-start.99
  731.0 7.0 copy-start.5
  738.1 7.3 copy-start.46
  792.6 146.7 %copy-start.55 = (f32[6912]{0:T(1024)S(1)}, f32[6912]{0:T(1024)}, u32[]{:S(2)}) copy-start(f32[6912]{0:T(1024)} %copy-done.54) | copy-start | bytes 82948
  792.6 163.6 %copy-start.49 = (bf16[1,16,6912]{2,0,1:T(2,128)(2,1)S(1)}, bf16[1,16,6912]{2,0,1:T(2,128)(2,1)}, u32[]{:S(2)}) copy-start(bf16[1,16,6912]{2,0,1:T(2,128)(2,1)} %copy-done.47) | copy-start | bytes 663556
  792.6 163.9 %copy-start.39 = (bf16[1152,16]{1,0:T(8,128)(2,1)S(1)}, bf16[1152,16]{1,0:T(8,128)(2,1)}, u32[]{:S(2)}) copy-start(bf16[1152,16]{1,0:T(8,128)(2,1)} %copy-done.38) | copy-start | bytes 110596
  792.7 210.9 %all-reduce.4.cloned.1.call-start = ((), (), s32[]{:S(2)}) async-start(), calls=%async_computation.12 | async-start | bytes 3391488 | tf_op jit(solution)/shard_map/psum | solution.py:306
  957.0 15.5 %copy-start.74 = (bf16[1,1152]{1,0:T(2,128)(2,1)S(1)}, bf16[1,1152]{1,0:T(2,128)(2,1)}, u32[]{:S(2)}) copy-start(bf16[1,1152]{1,0:T(2,128)(2,1)} %param.13) | copy-start | bytes 6916
  957.0 15.5 %copy-start.76 = (f32[1,1152]{1,0:T(1,128)S(1)}, f32[1,1152]{1,0:T(1,128)}, u32[]{:S(2)}) copy-start(f32[1,1152]{1,0:T(1,128)} %get-tuple-element.24) | copy-start | bytes 13828
  957.0 46.5 %copy-start.10 = (f32[423936]{0:T(1024)S(1)}, f32[423936]{0:T(1024)}, u32[]{:S(2)}) copy-start(f32[423936]{0:T(1024)} %param.20) | copy-start | bytes 5087236
  957.0 46.5 %copy-start.30 = (f32[423936]{0:T(1024)S(1)}, f32[423936]{0:T(1024)}, u32[]{:S(2)}) copy-start(f32[423936]{0:T(1024)} %param.21) | copy-start | bytes 5087236
  (86 other events, 242.6 us)
Sparse Core Ops, SparseCore 0:
  10.2 71.4 all-gather.10
  83.3 142.6 all-gather.8
  227.7 76.6 all-gather.12
  306.0 98.9 all-gather.22
  407.2 35.6 all-gather.16
  445.2 37.3 all-gather.14
  484.2 33.9 all-gather.18
  519.9 99.5 all-gather.20
  660.2 35.6 reduce-scatter.4
  698.8 37.3 reduce-scatter.2
  792.7 144.0 all-reduce.5
  940.4 63.0 all-reduce.3
where the time goes:
time: 1030 us; the launch traced here: 1020 us
  waiting for transfers between devices  658 us (64%)
  matrix products  148 us (14%)
  local copies, waits for them, and re-layouts  109 us (11%)
  other arithmetic  66.9 us (6%)
  blocking collectives  16.9 us (2%)
  between operations  16.7 us (2%)
    unnamed x13, waiting for transfers between devices  146 us
    all_gather x1, waiting for transfers between devices, shards(): lax.all_gather(weight_mod, 'fsdp', axis=0, tiled=True)  121 us
    all_gather x1, waiting for transfers between devices, shards(): expand = lax.all_gather(weight_fc1, 'fsdp', axis=0, tiled=True)  95.7 us
    all_gather x1, waiting for transfers between devices, shards(): lax.all_gather(weight_qkv, 'fsdp', axis=0, tiled=True)  68.8 us
    all_gather x1, waiting for transfers between devices, shards(): lax.all_gather(master.astype(jnp.bfloat16), 'fsdp', axis=0, tiled=True)  66.5 us
    all_gather x1, waiting for transfers between devices, shards(): contract = lax.all_gather(weight_fc2, 'fsdp', axis=0, tiled=True)  52.9 us
    all_gather x1, waiting for transfers between devices, shards(): lax.all_gather(values, 'rep', axis=1, tiled=True)  35.3 us
    slice x13, local copies, waits for them, and re-layouts, unpack(): tables.append(flat[offset:offset + count].reshape(shape))  31.5 us
  transfers between devices with their start and end apart: 12, of which 10 were waited for; matrix products, arithmetic and copies ran while one was open for 22% of the time, Pallas kernels for 0%

commit v1 on v0

--- a/solution.py
+++ b/solution.py
@@ -11,6 +11,25 @@
 STEP = 3
 adapter_scale = 2.0
 norm_eps = 1e-06
+
+
+def meet_sites_over_axis(own_rows, join_dim):
+    total_devices = lax.axis_size("rep")
+    gallery = [(s, (s + 1) % total_devices) for s in range(total_devices)]
+    ledger = [(s, (s - 1) % total_devices) for s in range(total_devices)]
+    ready, right_arr = ([own_rows], [own_rows])
+    for _ in range(total_devices // 2):
+        ready.append(lax.ppermute(ready[-1], "rep", gallery))
+    q = 0
+    while q < (total_devices - 1) // 2:
+        right_arr.append(lax.ppermute(right_arr[-1], "rep", ledger))
+        q = q + 1
+    tall = jnp.roll(
+        jnp.concatenate([*ready[::-1], *right_arr[1:]], axis=join_dim),
+        (lax.axis_index("rep") - total_devices // 2) * own_rows.shape[join_dim],
+        axis=join_dim,
+    )
+    return tall
 
 
 def adapter_shapes():
@@ -150,7 +169,7 @@
     keys = qkv_low[..., width : 2 * width]
     values = qkv_low[..., 2 * width :]
     keys_all, values_all = (
-        lax.all_gather(keys, "rep", axis=1, tiled=True),
+        meet_sites_over_axis(keys, join_dim=1),
         lax.all_gather(values, "rep", axis=1, tiled=True),
     )
     length = keys_all.shape[1]

time: 1030 us -> 989 us (0.960)
  waiting for transfers between devices: 658 us -> 600 us
    all_gather x1, waiting for transfers between devices: 52.9 us -> 3.34 us  [shards(): contract = lax.all_gather(weight_fc2, 'fsdp', axis=0, tiled=True)]
    ppermute x0 -> x3, waiting for transfers between devices: none -> 40 us  [the longest x2 29.1 us: meet_sites_over_axis(): ready.append(lax.ppermute(ready[-1], 'rep', gallery))]
    all_gather x1, waiting for transfers between devices: 35.3 us -> 6.74 us  [shards(): lax.all_gather(values, 'rep', axis=1, tiled=True)]
    all_gather x1 -> x0, waiting for transfers between devices: 25.6 us -> none  [shards(): lax.all_gather(keys, 'rep', axis=1, tiled=True)]
    unnamed x257 -> x258, local copies, waits for them, and re-layouts: 19.4 us -> 22.4 us
    unnamed x13 -> x12, waiting for transfers between devices: 146 us -> 146 us
  transfers between devices with their start and end apart: 12 -> 14, of which waited for: 10 -> 12; matrix products, arithmetic and copies ran while one was open for 22% -> 24% of each run, Pallas kernels for 0% -> 0%
where the time goes in v1:
time: 989 us; the launch traced here: 977 us
  waiting for transfers between devices  600 us (61%)
  matrix products  155 us (16%)
  local copies, waits for them, and re-layouts  116 us (12%)
  other arithmetic  66.9 us (7%)
  blocking collectives  17 us (2%)
  between operations  16.6 us (2%)
    unnamed x12, waiting for transfers between devices  146 us
    all_gather x1, waiting for transfers between devices, shards(): lax.all_gather(weight_mod, 'fsdp', axis=0, tiled=True)  121 us
    all_gather x1, waiting for transfers between devices, shards(): expand = lax.all_gather(weight_fc1, 'fsdp', axis=0, tiled=True)  95.7 us
    all_gather x1, waiting for transfers between devices, shards(): lax.all_gather(weight_qkv, 'fsdp', axis=0, tiled=True)  68.8 us
    all_gather x1, waiting for transfers between devices, shards(): lax.all_gather(master.astype(jnp.bfloat16), 'fsdp', axis=0, tiled=True)  66.4 us
    slice x13, local copies, waits for them, and re-layouts, unpack(): tables.append(flat[offset:offset + count].reshape(shape))  33.7 us
    psum x1, waiting for transfers between devices, shards(): grad = lax.psum(grad, 'rep')  30.5 us
    ppermute x2, waiting for transfers between devices, meet_sites_over_axis(): ready.append(lax.ppermute(ready[-1], 'rep', gallery))  29.1 us
  transfers between devices with their start and end apart: 14, of which 12 were waited for; matrix products, arithmetic and copies ran while one was open for 24% of the time, Pallas kernels for 0%

profile of v1, /device:TPU:0, one launch (start us, length us, event | category | flops | bytes accessed | tf_op | source)
XLA Modules:
  0.0 976.9 jit_solution(16137583799815270778)
XLA Ops:
  15.3 66.4 %all-gather.10.cloned.1.call-done = bf16[3391488]{0:T(1024)(128)(2,1)} async-done(((bf16[423936]{0:T(1024)(128)(2,1)}), bf16[3391488]{0:T(1024)(128)(2,1)}) %all-gather.10.cloned.1.call-update) | async-done | bytes 6782992 | tf_op jit(solution)/shard_map/all_gather | solution.py:83
  87.6 3.7 reshape.802
  104.7 121.3 %all-gather.8.cloned.1.call-done = bf16[1152,6912]{1,0:T(8,128)(2,1)} async-done(((bf16[144,6912]{1,0:T(8,128)(2,1)}), bf16[1152,6912]{1,0:T(8,128)(2,1)}) %all-gather.8.cloned.1.call-update) | async-done | bytes 15925264 | tf_op jit(solution)/shard_map/all_gather | solution.py:149
  226.1 7.7 convolution_reduce_fusion
  235.7 68.8 %all-gather.12.cloned.1.call-done = bf16[1152,3456]{1,0:T(8,128)(2,1)} async-done(((bf16[144,3456]{1,0:T(8,128)(2,1)}), bf16[1152,3456]{1,0:T(8,128)(2,1)}) %all-gather.12.cloned.1.call-update) | async-done | bytes 7962640 | tf_op jit(solution)/shard_map/all_gather | solution.py:160
  304.5 5.8 fusion.110
  312.5 14.9 %collective-permute-done = bf16[1,256,1152]{2,1,0:T(8,128)(2,1)S(1)} collective-permute-done((bf16[1,256,1152]{2,1,0:T(8,128)(2,1)S(1)}, bf16[1,256,1152]{2,1,0:T(8,128)(2,1)S(1)}, u32[]{:S(2)}, u32[]{:S(2)}) %collective-permute-start) | collective-permute-done | bytes 589856 | tf_op jit(solution)/shard_map/ppermute | solution.py:22
  330.4 14.2 %collective-permute-done.1 = bf16[1,256,1152]{2,1,0:T(8,128)(2,1)S(1)} collective-permute-done((bf16[1,256,1152]{2,1,0:T(8,128)(2,1)S(1)}, bf16[1,256,1152]{2,1,0:T(8,128)(2,1)S(1)}, u32[]{:S(2)}, u32[]{:S(2)}) %collective-permute-start.1) | collective-permute-done | bytes 589856 | tf_op jit(solution)/shard_map/ppermute | solution.py:22
  344.7 11.0 %collective-permute-done.2 = bf16[1,256,1152]{2,1,0:T(8,128)(2,1)S(1)} collective-permute-done((bf16[1,256,1152]{2,1,0:T(8,128)(2,1)S(1)}, bf16[1,256,1152]{2,1,0:T(8,128)(2,1)S(1)}, u32[]{:S(2)}, u32[]{:S(2)}) %collective-permute-start.2) | collective-permute-done | bytes 589856 | tf_op jit(solution)/shard_map/ppermute | solution.py:25
  368.5 3.8 slice.177
  372.3 3.7 slice.172
  376.0 8.3 slice.182
  384.3 6.3 multiply_reduce_fusion
  401.6 3.3 all-gather.20.cloned.1.call-done
  405.0 12.3 %fusion.56 = f32[256,4608]{1,0:T(8,128)} fusion(bf16[4608,1152]{1,0:T(8,128)(2,1)} %all-gather.20.cloned.1.call-done, bf16[1,256,1152]{2,1,0:T(8,128)(2,1)S(1)} %copy-done.12, f32[1152]{0:T(1024)S(1)} %get-tuple-element.13), kind=kOutput, calls=%fused_computation.129 | convolution fusion | flops 2718793728 | bytes 15929856 | tf_op jit(solution)/shard_map/ste,de->std/dot_general | solution.py:138
  418.2 3.3 constant_dynamic-slice_fusion
  421.5 4.5 copy.47
  426.2 4.2 multiply_reduce_fusion.2
  430.4 3.7 exponential_reduce_fusion
  436.2 6.7 all-gather.14.cloned.1.call-done
  442.9 4.3 copy.45
  447.2 8.7 convolution_convert_fusion.1
  456.8 21.7 %all-gather.16.cloned.1.call-done = bf16[1152,1152]{1,0:T(8,128)(2,1)} async-done(((bf16[144,1152]{1,0:T(8,128)(2,1)}), bf16[1152,1152]{1,0:T(8,128)(2,1)}) %all-gather.16.cloned.1.call-update) | async-done | bytes 2654224 | tf_op jit(solution)/shard_map/all_gather | solution.py:161
  484.0 95.7 %all-gather.18.cloned.1.call-done = bf16[1152,4608]{1,0:T(8,128)(2,1)} async-done(((bf16[144,4608]{1,0:T(8,128)(2,1)}), bf16[1152,4608]{1,0:T(8,128)(2,1)}) %all-gather.18.cloned.1.call-update) | async-done | bytes 10616848 | tf_op jit(solution)/shard_map/all_gather | solution.py:195
  579.7 5.9 fusion.112
  587.9 6.8 fusion.11
  596.6 3.2 fusion.114
  610.2 10.5 %convolution_convert_fusion = bf16[16,72,1024]{2,1,0:T(8,128)(2,1)} fusion(bf16[256,16,72]{0,2,1:T(8,128)(2,1)} %bitcast.241, f32[16,256,1024]{2,1,0:T(8,128)} %copy-done, f32[16,256]{1,0:T(8,128)S(1)} %log_add_fusion), kind=kOutput, calls=%fused_computation.50 | convolution fusion | flops 617742336 | bytes 19742720 | tf_op jit(solution)/shard_map/hqk,qhe->khe/dot_general | solution.py:236
  620.8 12.9 %multiply_reduce_fusion.1 = (f32[16,256]{1,0:T(8,128)S(1)}, f32[16,256,1024]{2,1,0:T(8,128)}) fusion(f32[16,256,1024]{2,1,0:T(8,128)} %copy-done, f32[16,256]{1,0:T(8,128)S(1)} %log_add_fusion, bf16[256,16,72]{0,2,1:T(8,128)(2,1)} %bitcast.242, bf16[1024,16,72]{0,2,1:T(8,128)(2,1)} %bitcast.233), kind=kOutput, calls=%fused_computation.3 | convolution fusion | flops 620752896 | bytes 36536320 | tf_op jit(solution)/shard_map/qhe,khe->hqk/dot_general | solution.py:240
  633.7 12.3 %multiply_convert_fusion.1 = bf16[16,256,1024]{2,1,0:T(8,128)(2,1)S(1)} fusion(f32[16,256,1024]{2,1,0:T(8,128)} %get-tuple-element.61, f32[16,256,1024]{2,1,0:T(8,128)} %copy-done, f32[16,256]{1,0:T(8,128)S(1)} %get-tuple-element.60, f32[16,256]{1,0:T(8,128)S(1)} %log_add_fusion), kind=kLoop, calls=%fused_computation.2 | loop fusion | flops 20971520 | bytes 41975808 | tf_op jit(solution)/shard_map/convert_element_type | solution.py:244
  646.0 3.6 multiply_convert_fusion.6
  657.2 3.5 reshape.825
  664.6 3.9 reshape.824
  668.5 3.9 reshape.821
  675.1 5.3 multiply_convert_fusion
  680.3 11.3 %reshape.827 = bf16[589824]{0:T(1024)(128)(2,1)} reshape(bf16[8,4608,16]{2,1,0:T(8,128)(2,1)} %multiply_convert_fusion) | data formatting | bytes 2359296 | tf_op jit(solution)/shard_map/reshape | solution.py:311
  691.6 7.0 fusion.24
  698.7 7.2 fusion.113
  710.2 5.9 fusion.101
  720.1 4.0 fusion.33
  728.6 3.6 reshape.816
  732.5 3.5 multiply_convert_fusion.4
  736.0 3.5 reshape.818
  755.2 142.4 %all-reduce.6.cloned.1.call-done = bf16[3391488]{0:T(1024)(128)(2,1)} async-done(((bf16[3391488]{0:T(1024)(128)(2,1)}), bf16[3391488]{0:T(1024)(128)(2,1)}) %all-reduce.6.cloned.1.call-update) | async-done | bytes 6782992
  900.0 17.0 %psum.14 = f32[6912]{0:T(1024)S(1)} all-reduce(f32[6912]{0:T(1024)S(1)} %copy-done.52), channel_id=1, replica_groups=mesh['rep'=4,'fsdp'=8] {'rep'}, use_global_device_ids=true, to_apply=%region_19.20 | all-reduce | flops 6912 | bytes 55296 | tf_op jit(solution)/shard_map/psum | solution.py:290
  917.9 15.4 %convolution_reduce_fusion.3 = f32[1152]{0:T(1024)S(1)} fusion(f32[6912,1]{0,1:T(1,128)S(1)} %reshape.860, bf16[1152,6912]{1,0:T(8,128)(2,1)} %all-gather.8.cloned.1.call-done), kind=kOutput, calls=%fused_computation.110 | convolution fusion | flops 95551488 | bytes 15957504 | tf_op jit(solution)/shard_map/dot_general | solution.py:291
  934.0 30.5 %all-reduce.4.cloned.1.call-done = f32[423936]{0:T(1024)} async-done(((f32[423936]{0:T(1024)}), f32[423936]{0:T(1024)}) %all-reduce.4.cloned.1.call-update) | async-done | bytes 1695760 | tf_op jit(solution)/shard_map/psum | solution.py:325
  964.4 5.5 fusion.103
  (387 shorter events, 127.4 us)
Async XLA Ops:
  7.2 74.5 %all-gather.10.cloned.1.call-start = ((), (), s32[]{:S(2)}) async-start(), calls=%async_computation.3 | async-start | bytes 7630848 | tf_op jit(solution)/shard_map/all_gather | solution.py:83
  9.7 216.4 %all-gather.8.cloned.1.call-start = ((), (), s32[]{:S(2)}) async-start(), calls=%async_computation.2 | async-start | bytes 17915904 | tf_op jit(solution)/shard_map/all_gather | solution.py:149
  10.5 294.0 %all-gather.12.cloned.1.call-start = ((), (), s32[]{:S(2)}) async-start(), calls=%async_computation.4 | async-start | bytes 8957952 | tf_op jit(solution)/shard_map/all_gather | solution.py:160
  11.2 393.8 %all-gather.20.cloned.1.call-start = ((), (), s32[]{:S(2)}) async-start(), calls=%async_computation.8 | async-start | bytes 11943936 | tf_op jit(solution)/shard_map/all_gather | solution.py:201
  11.8 431.2 %all-gather.14.cloned.1.call-start = ((), (), s32[]{:S(2)}) async-start(), calls=%async_computation.5 | async-start | bytes 2949120 | tf_op jit(solution)/shard_map/all_gather | solution.py:173
  12.0 222.5 %copy-start.75 = (f32[256]{0:T(256)}, f32[256]{0:T(256)S(1)}, u32[]{:S(2)}) copy-start(f32[256]{0:T(256)S(1)} %broadcast_multiply_fusion.2) | copy-start | bytes 3076
  12.3 72.4 %copy-start.91 = (f32[256]{0:T(256)}, f32[256]{0:T(256)S(1)}, u32[]{:S(2)}) copy-start(f32[256]{0:T(256)S(1)} %fusion.30) | copy-start | bytes 3076
  104.0 206.2 %copy-start.42 = (bf16[1,16,3456]{2,0,1:T(2,128)(2,1)}, bf16[1,16,3456]{2,0,1:T(2,128)(2,1)S(1)}, u32[]{:S(2)}) copy-start(bf16[1,16,3456]{2,0,1:T(2,128)(2,1)S(1)} %fusion.48) | copy-start | bytes 331780
  104.7 130.7 %copy-start.23 = (bf16[1152,16]{1,0:T(8,128)(2,1)}, bf16[1152,16]{1,0:T(8,128)(2,1)S(1)}, u32[]{:S(2)}) copy-start(bf16[1152,16]{1,0:T(8,128)(2,1)S(1)} %multiply_reduce_fusion.5) | copy-start | bytes 110596
  104.7 130.4 %copy-start.83 = (f32[256]{0:T(256)S(1)}, f32[256]{0:T(256)}, u32[]{:S(2)}) copy-start(f32[256]{0:T(256)} %fusion.81) | copy-start | bytes 3076
  234.5 170.5 %copy-start.66 = (f32[1152]{0:T(1024)}, f32[1152]{0:T(1024)S(1)}, u32[]{:S(2)}) copy-start(f32[1152]{0:T(1024)S(1)} %get-tuple-element.13) | copy-start | bytes 13828
  235.4 74.8 %copy-start.15 = (bf16[256,1152]{1,0:T(8,128)(2,1)}, bf16[256,1152]{1,0:T(8,128)(2,1)S(1)}, u32[]{:S(2)}) copy-start(bf16[256,1152]{1,0:T(8,128)(2,1)S(1)} %fusion.53) | copy-start | bytes 1769476
  235.7 74.6 %copy-start.77 = (bf16[256,16]{0,1:T(8,128)(2,1)}, bf16[256,16]{0,1:T(8,128)(2,1)S(1)}, u32[]{:S(2)}) copy-start(bf16[256,16]{0,1:T(8,128)(2,1)S(1)} %convolution_convert_fusion.4) | copy-start | bytes 24580
  311.0 16.4 %collective-permute-start = (bf16[1,256,1152]{2,1,0:T(8,128)(2,1)S(1)}, bf16[1,256,1152]{2,1,0:T(8,128)(2,1)S(1)}, u32[]{:S(2)}, u32[]{:S(2)}) collective-permute-start(bf16[1,256,1152]{2,1,0:T(8,128)(2,1)S(1)} %slice.196), channel_id=1, source_target_pairs={{0,8},{8,16},{16,24},{24,0},{1,9},{9,17},{17,25},{25,1},{2,10},{10... | collective-permute-start | bytes 1769480 | tf_op jit(solution)/shard_map/ppermute | solution.py:22
  327.4 17.1 %collective-permute-start.1 = (bf16[1,256,1152]{2,1,0:T(8,128)(2,1)S(1)}, bf16[1,256,1152]{2,1,0:T(8,128)(2,1)S(1)}, u32[]{:S(2)}, u32[]{:S(2)}) collective-permute-start(bf16[1,256,1152]{2,1,0:T(8,128)(2,1)S(1)} %collective-permute-done), channel_id=1, source_target_pairs={{0,8},{8,16},{16,24},{24,0},{1,9},{9,17},{17,25},{25,1},{2,10},{10... | collective-permute-start | bytes 1769480 | tf_op jit(solution)/shard_map/ppermute | solution.py:22
  328.0 27.7 %collective-permute-start.2 = (bf16[1,256,1152]{2,1,0:T(8,128)(2,1)S(1)}, bf16[1,256,1152]{2,1,0:T(8,128)(2,1)S(1)}, u32[]{:S(2)}, u32[]{:S(2)}) collective-permute-start(bf16[1,256,1152]{2,1,0:T(8,128)(2,1)S(1)} %slice.196), channel_id=1, source_target_pairs={{0,24},{8,0},{16,8},{24,16},{1,25},{9,1},{17,9},{25,17},{2,26},{10... | collective-permute-start | bytes 1769480 | tf_op jit(solution)/shard_map/ppermute | solution.py:25
  359.3 119.2 %all-gather.16.cloned.1.call-start = ((), (), s32[]{:S(2)}) async-start(), calls=%async_computation.6 | async-start | bytes 2985984 | tf_op jit(solution)/shard_map/all_gather | solution.py:161
  359.8 219.9 %all-gather.18.cloned.1.call-start = ((), (), s32[]{:S(2)}) async-start(), calls=%async_computation.7 | async-start | bytes 11943936 | tf_op jit(solution)/shard_map/all_gather | solution.py:195
  360.6 345.4 %reduce-scatter.5.cloned.1.call-start = ((), (), s32[]{:S(2)}) async-start(), calls=%async_computation.10 | async-start | bytes 2949120 | tf_op jit(solution)/shard_map/reduce_scatter | solution.py:261
  368.5 7.5 copy-start.21
  376.0 8.3 copy-start.106
  390.6 7.4 copy-start.105
  392.9 7.9 copy-start.55
  398.6 57.3 %copy-start.25 = (bf16[1152,16]{1,0:T(8,128)(2,1)}, bf16[1152,16]{1,0:T(8,128)(2,1)S(1)}, u32[]{:S(2)}) copy-start(bf16[1152,16]{1,0:T(8,128)(2,1)S(1)} %multiply_reduce_fusion.4) | copy-start | bytes 110596
  455.9 25.4 %copy-start.10 = (bf16[16,72,256]{2,1,0:T(8,128)(2,1)}, bf16[16,72,256]{2,1,0:T(8,128)(2,1)S(1)}, u32[]{:S(2)}) copy-start(bf16[16,72,256]{2,1,0:T(8,128)(2,1)S(1)} %convolution_convert_fusion.1) | copy-start | bytes 1769476
  483.7 101.9 %copy-start.17 = (bf16[256,1152]{1,0:T(8,128)(2,1)}, bf16[256,1152]{1,0:T(8,128)(2,1)S(1)}, u32[]{:S(2)}) copy-start(bf16[256,1152]{1,0:T(8,128)(2,1)S(1)} %fusion.50) | copy-start | bytes 1769476
  484.0 101.6 %copy-start.40 = (bf16[1,16,4608]{2,0,1:T(2,128)(2,1)S(1)}, bf16[1,16,4608]{2,0,1:T(2,128)(2,1)}, u32[]{:S(2)}) copy-start(bf16[1,16,4608]{2,0,1:T(2,128)(2,1)} %fusion.38) | copy-start | bytes 442372
  585.7 10.9 %slice-start.1 = ((s8[10616832]{0:T(1024)(128)(4,1)}), s8[4194304]{0:T(1024)(128)(4,1)S(1)}, s32[]{:S(2)}) async-start(s8[10616832]{0:T(1024)(128)(4,1)} %bitcast.247), calls=%async_computation.14 | async-start | bytes 8388608
  587.8 15.8 %copy-start.3 = (bf16[256,4608]{1,0:T(8,128)(2,1)}, bf16[256,4608]{1,0:T(8,128)(2,1)S(1)}, u32[]{:S(2)}) copy-start(bf16[256,4608]{1,0:T(8,128)(2,1)S(1)} %get-tuple-element.57) | copy-start | bytes 7077892
  587.8 8.7 slice-start.2
  587.9 8.7 slice-start.3
  620.7 85.3 %reduce-scatter.3.cloned.1.call-start = ((), (), s32[]{:S(2)}) async-start(), calls=%async_computation.9 | async-start | bytes 2949120 | tf_op jit(solution)/shard_map/reduce_scatter | solution.py:258
  651.4 246.2 %all-reduce.6.cloned.1.call-start = ((), (), s32[]{:S(2)}) async-start(), calls=%async_computation.12 | async-start | bytes 13565952
  652.4 8.3 copy-start.18
  652.4 8.3 copy-start.61
  653.1 8.0 copy-start.11
  653.1 8.0 copy-start.63
  664.6 7.9 copy-start.96
  691.6 7.0 copy-start.4
  698.7 7.3 copy-start.43
  753.3 146.7 %copy-start.52 = (f32[6912]{0:T(1024)S(1)}, f32[6912]{0:T(1024)}, u32[]{:S(2)}) copy-start(f32[6912]{0:T(1024)} %copy-done.51) | copy-start | bytes 82948
  753.3 163.8 %copy-start.46 = (bf16[1,16,6912]{2,0,1:T(2,128)(2,1)S(1)}, bf16[1,16,6912]{2,0,1:T(2,128)(2,1)}, u32[]{:S(2)}) copy-start(bf16[1,16,6912]{2,0,1:T(2,128)(2,1)} %copy-done.44) | copy-start | bytes 663556
  753.3 164.1 %copy-start.36 = (bf16[1152,16]{1,0:T(8,128)(2,1)S(1)}, bf16[1152,16]{1,0:T(8,128)(2,1)}, u32[]{:S(2)}) copy-start(bf16[1152,16]{1,0:T(8,128)(2,1)} %copy-done.35) | copy-start | bytes 110596
  753.3 211.1 %all-reduce.4.cloned.1.call-start = ((), (), s32[]{:S(2)}) async-start(), calls=%async_computation.11 | async-start | bytes 3391488 | tf_op jit(solution)/shard_map/psum | solution.py:325
  917.8 15.5 %copy-start.71 = (bf16[1,1152]{1,0:T(2,128)(2,1)S(1)}, bf16[1,1152]{1,0:T(2,128)(2,1)}, u32[]{:S(2)}) copy-start(bf16[1,1152]{1,0:T(2,128)(2,1)} %param.13) | copy-start | bytes 6916
  917.8 15.5 %copy-start.73 = (f32[1,1152]{1,0:T(1,128)S(1)}, f32[1,1152]{1,0:T(1,128)}, u32[]{:S(2)}) copy-start(f32[1,1152]{1,0:T(1,128)} %get-tuple-element.24) | copy-start | bytes 13828
  917.8 46.6 %copy-start.9 = (f32[423936]{0:T(1024)S(1)}, f32[423936]{0:T(1024)}, u32[]{:S(2)}) copy-start(f32[423936]{0:T(1024)} %param.20) | copy-start | bytes 5087236
  917.9 46.6 %copy-start.31 = (f32[423936]{0:T(1024)S(1)}, f32[423936]{0:T(1024)}, u32[]{:S(2)}) copy-start(f32[423936]{0:T(1024)} %param.21) | copy-start | bytes 5087236
  (85 other events, 245.1 us)
Sparse Core Ops, SparseCore 0:
  10.2 71.4 all-gather.9
  83.3 142.6 all-gather.7
  227.7 76.6 all-gather.11
  306.0 98.9 all-gather.19
  407.2 35.6 all-gather.13
  444.4 33.9 all-gather.15
  480.1 99.5 all-gather.17
  620.8 35.6 reduce-scatter.4
  659.6 37.3 reduce-scatter.2
  753.4 144.0 all-reduce.5
  901.3 63.0 all-reduce.3
